TPU v7x, 32 devices: a whole 2x2x4 slice. The times are simulated.
32 devices in a mesh: dp: 4 (over x, core), param: 8 (over z, y).
Axes of the slice: x: 2, y: 2, z: 4, core: 2. Of those that a mesh axis runs over, the one named last changes fastest.
Arguments:
- train_grads: bfloat16 [3584, 212992], P('dp', 'param'), as said below
- query_grads: bfloat16 [128, 212992], P('dp', 'param'), as said below
Outputs:
- scores: float32 [128, 3584], P('param', 'dp')
Inputs may be any that keep to these rules, and one draw needn't show every extreme that they name: `train_grads`: finite real values. `query_grads`: finite real values.
All inputs are finite; a program needn't handle non-finite values.
Results may differ from a plain program's by a relative error of at most 0.0003.
Values may be sent and summed in bfloat16 or wider, within the bound.
A program may use at most 128 MiB of HBM per device.

v0:
```python
import jax
import jax.numpy as jnp
from jax import lax
from jax.sharding import PartitionSpec as P

epsilon = 1e-06


def per_device(train_grads, query_grads):
    queries = lax.all_gather(query_grads, "dp", axis=0, tiled=True)
    products = lax.dot_general(
        queries, train_grads, (((1,), (1,)), ((), ())), preferred_element_type=jnp.float32
    )
    query_norm = jnp.sum(jnp.square(queries.astype(jnp.float32)), axis=1)
    train_norm = jnp.sum(jnp.square(train_grads.astype(jnp.float32)), axis=1)
    products, query_norm = (
        lax.psum_scatter(products, "param", scatter_dimension=0, tiled=True),
        lax.psum_scatter(query_norm, "param", scatter_dimension=0, tiled=True),
    )
    train_norm = lax.psum(train_norm, "param")
    return (
        products
        * lax.rsqrt(query_norm + epsilon)[:, None]
        * lax.rsqrt(train_norm + epsilon)[None, :]
    )


def solution(mesh):
    return jax.shard_map(
        per_device,
        mesh=mesh,
        in_specs=(P("dp", "param"), P("dp", "param")),
        out_specs=P("param", "dp"),
        check_vma=False,
    )
```

profile of v0, /device:TPU:0, one launch (start us, length us, event | category | flops | bytes accessed | tf_op | source)
XLA Modules:
  0.0 154.5 jit_solution(13825321456841834263)
XLA Ops:
  6.5 0.0 all-gather.2.cloned.1.call-start
  6.5 0.7 all-gather.2.cloned.1.call-update
  7.3 0.0 reduce-scatter.2.cloned.1.call-start
  7.3 53.7 %all-gather.2.cloned.1.call-done = bf16[128,26624]{1,0:T(8,128)(2,1)} async-done(((bf16[32,26624]{1,0:T(8,128)(2,1)}), bf16[128,26624]{1,0:T(8,128)(2,1)}) %all-gather.2.cloned.1.call-update) | async-done | bytes 6815760 | tf_op jit(solution)/shard_map/all_gather | solution.py:10
  61.0 22.4 %fusion.1 = f32[128,896]{1,0:T(8,128)} fusion(bf16[128,26624]{1,0:T(8,128)(2,1)} %all-gather.2.cloned.1.call-done, bf16[896,26624]{1,0:T(8,128)(2,1)} %param.2), kind=kOutput, calls=%fused_computation.6 | convolution fusion | flops 6106906624 | bytes 54984704 | tf_op jit(solution)/shard_map/dot_general | solution.py:11
  83.4 0.0 reduce-scatter.2.cloned.1.call-update
  83.5 0.0 copy-start
  83.5 16.4 %multiply_reduce_fusion = f32[896]{0:T(1024)S(1)} fusion(bf16[896,26624]{1,0:T(8,128)(2,1)} %param.2), kind=kLoop, calls=%fused_computation | loop fusion | flops 71564416 | bytes 47713792 | tf_op jit(solution)/shard_map/reduce_sum | solution.py:15
  99.8 0.0 copy-done
  99.8 0.6 dynamic-slice
  101.1 4.4 %multiply_reduce_fusion.1 = f32[128]{0:T(128)S(1)} fusion(bf16[128,26624]{1,0:T(8,128)(2,1)} %all-gather.2.cloned.1.call-done), kind=kLoop, calls=%fused_computation.1 | loop fusion | flops 10223488 | bytes 6816256 | tf_op jit(solution)/shard_map/reduce_sum | solution.py:14
  105.5 21.6 %all-reduce.1 = (f32[896]{0:T(1024)S(1)}, f32[128]{0:T(128)S(1)}) all-reduce(f32[896]{0:T(1024)S(1)} %multiply_reduce_fusion, f32[128]{0:T(128)S(1)} %multiply_reduce_fusion.1), channel_id=1, replica_groups=mesh['dp'=4,'param'=8] {'param'}, use_global_device_ids=true, to_apply=%region_4.0 | all-reduce | flops 1024 | bytes 8192 | tf_op jit(solution)/shard_map/psum | solution.py:20
  127.1 0.1 fusion
  127.1 19.0 %reduce-scatter.2.cloned.1.call-done = f32[16,896]{1,0:T(8,128)} async-done(((f32[128,896]{1,0:T(8,128)}), f32[16,896]{1,0:T(8,128)}) %reduce-scatter.2.cloned.1.call-update) | async-done | bytes 57360 | tf_op jit(solution)/shard_map/reduce_scatter | solution.py:17
  146.2 1.5 multiply_multiply_fusion
  (1 shorter events, 0.0 us)
Async XLA Ops:
  6.5 54.4 %all-gather.2.cloned.1.call-start = ((), (), s32[]{:S(2)}) async-start(), calls=%async_computation.1 | async-start | bytes 8519680 | tf_op jit(solution)/shard_map/all_gather | solution.py:10
  7.3 138.9 %reduce-scatter.2.cloned.1.call-start = ((), (), s32[]{:S(2)}) async-start(), calls=%async_computation.2 | async-start | bytes 516096 | tf_op jit(solution)/shard_map/reduce_scatter | solution.py:17
  83.5 16.4 %copy-start = (u32[32]{0:T(128)S(1)}, u32[32]{0:T(128)}, u32[]{:S(2)}) copy-start(u32[32]{0:T(128)} %constant.7) | copy-start | bytes 388
Sparse Core Ops, SparseCore 0:
  8.9 52.0 all-gather.1
  83.6 62.5 reduce-scatter.1
where the time goes:
time: 155 us
  waiting for transfers between devices  73.4 us (47%)
  matrix products  22.4 us (14%)
  other arithmetic  22.4 us (14%)
  blocking collectives  21.6 us (14%)
  between operations  14.1 us (9%)
    all_gather x1, waiting for transfers between devices, per_device(): queries = lax.all_gather(query_grads, 'dp', axis=0, tiled=True)  53.7 us
    dot_general x1, matrix products, per_device(): lax.dot_general(queries, train_grads, (((1,), (1,)), ((), ())), preferred...  22.4 us
    psum x1, blocking collectives, per_device(): train_norm = lax.psum(train_norm, 'param')  21.6 us
    reduce_scatter x1, waiting for transfers between devices, per_device(): lax.psum_scatter(products, 'param', scatter_dimension=0, tiled=True)  19 us
    reduce_sum x1, other arithmetic, per_device(): train_norm = jnp.sum(jnp.square(train_grads.astype(jnp.float32)), axis=1)  16.4 us
    reduce_sum x1, other arithmetic, per_device(): query_norm = jnp.sum(jnp.square(queries.astype(jnp.float32)), axis=1)  4.39 us
  transfers between devices with their start and end apart: 2, of which 2 were waited for; matrix products, arithmetic and copies ran while one was open for 14% of the time, Pallas kernels for 0%

commit v1 on v0

--- a/solution.py
+++ b/solution.py
@@ -7,7 +7,9 @@
 
 
 def per_device(train_grads, query_grads):
-    queries = lax.all_gather(query_grads, "dp", axis=0, tiled=True)
+    queries = jnp.concatenate(
+        lax.all_to_all(jnp.stack([query_grads] * lax.axis_size("dp")), "dp", 0, 0), axis=0
+    )
     products = lax.dot_general(
         queries, train_grads, (((1,), (1,)), ((), ())), preferred_element_type=jnp.float32
     )

time: 155 us -> 184 us (1.19)
  blocking collectives: 21.6 us -> 103 us
  waiting for transfers between devices: 73.4 us -> 18.8 us
  local copies, waits for them, and re-layouts: 0.59 us -> 2.78 us
    all_to_all x0 -> x1, blocking collectives: none -> 80.6 us  [per_device(): lax.all_to_all(jnp.stack([query_grads] * lax.axis_size('dp')), 'dp', 0, 0)]
    all_gather x1 -> x0, waiting for transfers between devices: 53.7 us -> none  [per_device(): queries = lax.all_gather(query_grads, 'dp', axis=0, tiled=True)]
    another operation x0 -> x1, local copies, waits for them, and re-layouts: none -> 2.11 us  [per_device(): jnp.stack([query_grads] * lax.axis_size('dp'))]
  transfers between devices with their start and end apart: 2 -> 1, of which waited for: 2 -> 1; matrix products, arithmetic and copies ran while one was open for 14% -> 12% of each run, Pallas kernels for 0% -> 0%
where the time goes in v1:
time: 184 us
  blocking collectives  103 us (56%)
  matrix products  22.4 us (12%)
  other arithmetic  22.4 us (12%)
  waiting for transfers between devices  18.8 us (10%)
  between operations  14.1 us (8%)
  local copies, waits for them, and re-layouts  2.78 us (2%)
    all_to_all x1, blocking collectives, per_device(): lax.all_to_all(jnp.stack([query_grads] * lax.axis_size('dp')), 'dp', 0, 0)  80.6 us
    psum x1, blocking collectives, per_device(): train_norm = lax.psum(train_norm, 'param')  22.6 us
    dot_general x1, matrix products, per_device(): lax.dot_general(queries, train_grads, (((1,), (1,)), ((), ())), preferred...  22.4 us
    reduce_scatter x1, waiting for transfers between devices, per_device(): lax.psum_scatter(products, 'param', scatter_dimension=0, tiled=True)  18.8 us
    reduce_sum x1, other arithmetic, per_device(): train_norm = jnp.sum(jnp.square(train_grads.astype(jnp.float32)), axis=1)  16.4 us
    reduce_sum x1, other arithmetic, per_device(): query_norm = jnp.sum(jnp.square(queries.astype(jnp.float32)), axis=1)  4.45 us
  transfers between devices with their start and end apart: 1, of which 1 were waited for; matrix products, arithmetic and copies ran while one was open for 12% of the time, Pallas kernels for 0%

profile of v1, /device:TPU:0, one launch (start us, length us, event | category | flops | bytes accessed | tf_op | source)
XLA Modules:
  0.0 183.7 jit_solution(11833250753314936203)
XLA Ops:
  6.5 0.0 reduce-scatter.2.cloned.1.call-start
  6.5 2.1 %stack.2 = bf16[4,32,26624]{2,1,0:T(8,128)(2,1)S(1)} broadcast(bf16[32,26624]{1,0:T(8,128)(2,1)} %param.3), dimensions={1,2} | broadcast | bytes 8519680 | tf_op jit(solution)/shard_map/stack | solution.py:11
  8.7 80.6 %all_to_all.5 = bf16[4,32,26624]{2,1,0:T(8,128)(2,1)} all-to-all(bf16[4,32,26624]{2,1,0:T(8,128)(2,1)S(1)} %stack.2), channel_id=1, replica_groups=mesh['dp'=4,'param'=8] {'dp'}, dimensions={0} | all-to-all | bytes 13631488 | tf_op jit(solution)/shard_map/all_to_all | solution.py:11
  89.2 22.4 %fusion.1 = f32[128,896]{1,0:T(8,128)} fusion(bf16[128,26624]{1,0:T(8,128)(2,1)} %bitcast.4, bf16[896,26624]{1,0:T(8,128)(2,1)} %param.2), kind=kOutput, calls=%fused_computation.6 | convolution fusion | flops 6106906624 | bytes 54984704 | tf_op jit(solution)/shard_map/dot_general | solution.py:13
  111.7 0.0 reduce-scatter.2.cloned.1.call-update
  111.7 0.0 copy-start
  111.7 16.4 %multiply_reduce_fusion = f32[896]{0:T(1024)S(1)} fusion(bf16[896,26624]{1,0:T(8,128)(2,1)} %param.2), kind=kLoop, calls=%fused_computation | loop fusion | flops 71564416 | bytes 47713792 | tf_op jit(solution)/shard_map/reduce_sum | solution.py:17
  128.1 0.0 copy-done
  128.1 0.6 dynamic-slice
  129.3 4.4 %multiply_reduce_fusion.1 = f32[4,32]{1,0:T(4,128)S(1)} fusion(bf16[4,32,26624]{2,1,0:T(8,128)(2,1)} %all_to_all.5), kind=kLoop, calls=%fused_computation.1 | loop fusion | flops 10223488 | bytes 6816256 | tf_op jit(solution)/shard_map/reduce_sum | solution.py:16
  133.8 0.1 reduce_sum.21
  133.9 22.6 %all-reduce.1 = (f32[896]{0:T(1024)S(1)}, f32[128]{0:T(128)S(1)}) all-reduce(f32[896]{0:T(1024)S(1)} %multiply_reduce_fusion, f32[128]{0:T(128)S(1)} %reduce_sum.21), channel_id=1, replica_groups=mesh['dp'=4,'param'=8] {'param'}, use_global_device_ids=true, to_apply=%region_4.0 | all-reduce | flops 1024 | bytes 8192 | tf_op jit(solution)/shard_map/psum | solution.py:22
  156.5 0.1 fusion
  156.6 18.8 %reduce-scatter.2.cloned.1.call-done = f32[16,896]{1,0:T(8,128)} async-done(((f32[128,896]{1,0:T(8,128)}), f32[16,896]{1,0:T(8,128)}) %reduce-scatter.2.cloned.1.call-update) | async-done | bytes 57360 | tf_op jit(solution)/shard_map/reduce_scatter | solution.py:19
  175.4 1.5 multiply_multiply_fusion
  (1 shorter events, 0.0 us)
Async XLA Ops:
  6.5 168.8 %reduce-scatter.2.cloned.1.call-start = ((), (), s32[]{:S(2)}) async-start(), calls=%async_computation.2 | async-start | bytes 516096 | tf_op jit(solution)/shard_map/reduce_scatter | solution.py:19
  111.7 16.4 %copy-start = (u32[32]{0:T(128)S(1)}, u32[32]{0:T(128)}, u32[]{:S(2)}) copy-start(u32[32]{0:T(128)} %constant.7) | copy-start | bytes 388
Sparse Core Ops, SparseCore 0:
  111.8 63.4 reduce-scatter.1
